TPU v7x, 32 devices: a whole 2x2x4 slice. The times are simulated.
32 devices in a mesh: col: 8 (over y, x, core), row: 4 (over z).
Axes of the slice: x: 2, y: 2, z: 4, core: 2. Of those that a mesh axis runs over, the one named last changes fastest.
Arguments:
- features: bfloat16 [65536, 2048], P(('col', 'row')), may hold values from -6 to 6
- leaf_in: bfloat16 [65536, 128], P(('col', 'row')), may hold values from -0.1875 to 0.1875
- mix_in: bfloat16 [3, 64, 128, 256], P(None, ('col', 'row')), may hold values from -0.375 to 0.375
- mix_out: bfloat16 [3, 64, 128, 256], P(None, 'col'), may hold values from -0.375 to 0.375
- leaf_out: bfloat16 [65536, 128], P('col'), may hold values from -0.5 to 0.5
Outputs:
- result: bfloat16 [65536, 2048], P(('col', 'row'))
All inputs are finite; a program needn't handle non-finite values.
Results may differ from a plain program's by a relative error of at most 0.023.
Values may be sent and summed in bfloat16 or wider, within the bound.
No kernel may reach another device: no remote copies, remote signals or barrier semaphores. Data moves between devices by JAX's collectives and lax.ppermute only.
A program may use at most 128 MiB of HBM per device.

v0:
```python
import jax
import jax.numpy as jnp
from jax import lax
from jax.sharding import PartitionSpec as P

LEAF_SIZE = 1024


def swapped(block, axis, stride):
    count = lax.axis_size(axis)
    route = []
    for low in range(count):
        high = low | 1 << stride
        if high != low and high < count:
            route += [(low, high), (high, low)]
    return lax.ppermute(block, axis, route)


def partner_of(coeffs, level_bit):
    total_blocks = coeffs.shape[0]
    shaped = coeffs.reshape(
        (total_blocks // (2 << level_bit), 2, 1 << level_bit) + coeffs.shape[1:]
    )
    return jnp.flip(shaped, 1).reshape(coeffs.shape)


def forward_mix(weights, coeffs, partner):
    stacked = jnp.concatenate([coeffs, partner], axis=1)
    return jnp.einsum("bkj,bjr->bkr", weights, stacked, preferred_element_type=jnp.float32).astype(
        jnp.bfloat16
    )


def backward_terms(weights, gradient):
    rank_size = gradient.shape[1]
    direct = jnp.einsum(
        "bjk,bjr->bkr", weights[:, :, :rank_size], gradient, preferred_element_type=jnp.float32
    )
    crossed = jnp.einsum(
        "bjk,bjr->bkr", weights[:, :, rank_size:], gradient, preferred_element_type=jnp.float32
    )
    return (direct, crossed.astype(jnp.bfloat16))


def body(features, leaf_in, mix_in, mix_out, leaf_out):
    rank_size = leaf_in.shape[1]
    side_count = features.shape[1]
    blocks = features.shape[0] // LEAF_SIZE
    col_bits = lax.axis_size("col").bit_length() - 1
    row_bits = lax.axis_size("row").bit_length() - 1
    feature_blocks = features.reshape(blocks, LEAF_SIZE, side_count)
    leaf_rows = leaf_in.reshape(blocks, LEAF_SIZE, rank_size)
    coeffs = jnp.einsum(
        "bmk,bmr->bkr", leaf_rows, feature_blocks, preferred_element_type=jnp.float32
    ).astype(jnp.bfloat16)
    for level_bit in range(col_bits):
        partner = swapped(coeffs, "col", level_bit)
        coeffs = forward_mix(mix_in[level_bit], coeffs, partner)
    coeffs = lax.all_to_all(coeffs, "row", split_axis=2, concat_axis=0, tiled=True)
    for level_bit in range(row_bits + 1):
        coeffs = forward_mix(mix_out[level_bit], coeffs, partner_of(coeffs, level_bit))
    out_rows = leaf_out.reshape(-1, LEAF_SIZE, rank_size)
    images = jnp.einsum(
        "bmk,bkr->bmr", out_rows, coeffs, preferred_element_type=jnp.float32
    ).astype(jnp.bfloat16)
    gradient = jnp.einsum(
        "bmk,bmr->bkr", out_rows, images, preferred_element_type=jnp.float32
    ).astype(jnp.bfloat16)
    for level_bit in reversed(range(row_bits + 1)):
        direct, crossed = backward_terms(mix_out[level_bit], gradient)
        gradient = (direct + partner_of(crossed, level_bit)).astype(jnp.bfloat16)
    gradient = lax.all_to_all(gradient, "row", split_axis=0, concat_axis=2, tiled=True)
    for level_bit in reversed(range(col_bits)):
        direct, crossed = backward_terms(mix_in[level_bit], gradient)
        gradient = (direct + swapped(crossed, "col", level_bit)).astype(jnp.bfloat16)
    result = jnp.einsum(
        "bmk,bkr->bmr", leaf_rows, gradient, preferred_element_type=jnp.float32
    ).astype(jnp.bfloat16)
    return result.reshape(features.shape)


def solution(mesh):
    in_specs = (
        P(("col", "row"), None),
        P(("col", "row"), None),
        P(None, ("col", "row"), None, None),
        P(None, "col", None, None),
        P("col", None),
    )
    out_specs = P(("col", "row"), None)
    return jax.shard_map(body, mesh=mesh, in_specs=in_specs, out_specs=out_specs, check_vma=False)
```

profile of v0, /device:TPU:0, one launch (start us, length us, event | category | flops | bytes accessed | tf_op | source)
XLA Modules:
  0.0 228.1 jit_solution(17529232885362974164)
XLA Ops:
  0.0 5.0 %convolution_convert_fusion.7 = bf16[2,128,2048]{2,1,0:T(8,128)(2,1)S(1)} fusion(bf16[2,1024,128]{2,1,0:T(8,128)(2,1)} %bitcast.112, bf16[2,1024,2048]{2,1,0:T(8,128)(2,1)} %bitcast.109), kind=kOutput, calls=%fused_computation.15 | convolution fusion | flops 1074266112 | bytes 9961472 | tf_op jit(solution)/shard_map/bmk,bmr->bkr/dot_general | solution.py:53
  5.6 2.3 %collective-permute-done = bf16[2,128,2048]{2,1,0:T(8,128)(2,1)S(1)} collective-permute-done((bf16[2,128,2048]{2,1,0:T(8,128)(2,1)S(1)}, bf16[2,128,2048]{2,1,0:T(8,128)(2,1)S(1)}, u32[]{:S(2)}, u32[]{:S(2)}) %collective-permute-start) | collective-permute-done | bytes 1048608 | tf_op jit(solution)/shard_map/ppermute | solution.py:16
  8.3 2.9 %collective-permute-start.1 = (bf16[2,128,2048]{2,1,0:T(8,128)(2,1)S(1)}, bf16[2,128,2048]{2,1,0:T(8,128)(2,1)S(1)}, u32[]{:S(2)}, u32[]{:S(2)}) collective-permute-start(bf16[2,128,2048]{2,1,0:T(8,128)(2,1)S(1)} %fusion.10), channel_id=1, source_target_pairs={{0,8},{8,0},{4,12},{12,4},{16,24},{24,16},{20,28},{28,20},{1,9},{9... | collective-permute-start | bytes 3145736 | tf_op jit(solution)/shard_map/ppermute | solution.py:16
  11.2 23.5 %collective-permute-done.1 = bf16[2,128,2048]{2,1,0:T(8,128)(2,1)S(1)} collective-permute-done((bf16[2,128,2048]{2,1,0:T(8,128)(2,1)S(1)}, bf16[2,128,2048]{2,1,0:T(8,128)(2,1)S(1)}, u32[]{:S(2)}, u32[]{:S(2)}) %collective-permute-start.1) | collective-permute-done | bytes 1048608 | tf_op jit(solution)/shard_map/ppermute | solution.py:16
  37.0 22.9 %collective-permute-done.2 = bf16[2,128,2048]{2,1,0:T(8,128)(2,1)S(1)} collective-permute-done((bf16[2,128,2048]{2,1,0:T(8,128)(2,1)S(1)}, bf16[2,128,2048]{2,1,0:T(8,128)(2,1)S(1)}, u32[]{:S(2)}, u32[]{:S(2)}) %collective-permute-start.2) | collective-permute-done | bytes 1048608 | tf_op jit(solution)/shard_map/ppermute | solution.py:16
  60.8 9.5 %copy.13 = bf16[2,128,2048]{1,0,2:T(2,128)(2,1)} copy(bf16[2,128,2048]{1,2,0:T(8,128)(2,1)S(1)} %fusion.9) | data formatting | bytes 2097152 | tf_op jit(solution)/shard_map/convert_element_type | solution.py:29
  70.3 4.8 %all-to-all-start = ((bf16[2,128,2048]{1,0,2:T(2,128)(2,1)}), bf16[2,128,2048]{1,0,2:T(2,128)(2,1)S(1)}, u32[]{:S(2)}, u32[]{:S(2)}) async-start(bf16[2,128,2048]{1,0,2:T(2,128)(2,1)} %copy.13), calls=%async_computation | async-start | bytes 2097152 | tf_op jit(solution)/shard_map/all_to_all | solution.py:59
  75.1 2.6 %slice_bitcast_fusion.2 = (bf16[8,128,256]{2,1,0:T(8,128)(2,1)}, bf16[8,128,256]{2,1,0:T(8,128)(2,1)}, bf16[8,128,256]{2,1,0:T(8,128)(2,1)}) fusion(bf16[3,8,128,256]{3,2,1,0:T(8,128)(2,1)} %param.8), kind=kLoop, calls=%fused_computation.60 | loop fusion | bytes 3145728 | tf_op jit(solution)/shard_map/squeeze | solution.py:70
  77.7 21.8 %all-to-all-done = bf16[2,128,2048]{1,0,2:T(2,128)(2,1)S(1)} async-done(((bf16[2,128,2048]{1,0,2:T(2,128)(2,1)}), bf16[2,128,2048]{1,0,2:T(2,128)(2,1)S(1)}, u32[]{:S(2)}, u32[]{:S(2)}) %all-to-all-start) | async-done | bytes 1048608 | tf_op jit(solution)/shard_map/all_to_all | solution.py:59
  101.4 2.4 %reverse.3 = bf16[4,2,128,512]{3,2,1,0:T(8,128)(2,1)} reverse(bf16[4,2,128,512]{3,2,1,0:T(8,128)(2,1)} %bitcast.119), dimensions={1} | reverse | bytes 2097152 | tf_op jit(solution)/shard_map/reverse
  103.8 2.8 %fusion.42 = bf16[8,512,128]{1,2,0:T(8,128)(2,1)} fusion(bf16[8,128,512]{2,1,0:T(8,128)(2,1)} %bitcast.128, bf16[8,128,512]{2,1,0:T(8,128)(2,1)S(1)} %bitcast.120, bf16[3,8,128,256]{3,2,1,0:T(8,128)(2,1)} %param.8), kind=kOutput, calls=%fused_computation.53 | convolution fusion | flops 273154048 | bytes 3670016 | tf_op jit(solution)/shard_map/bkj,bjr->bkr/dot_general | solution.py:29
  106.6 2.4 %rev.19 = bf16[2,2,2,128,512]{4,3,2,1,0:T(8,128)(2,1)} reverse(bf16[2,2,2,128,512]{4,3,2,1,0:T(8,128)(2,1)} %bitcast.124), dimensions={1} | reverse | bytes 2097152 | tf_op jit(solution)/shard_map/jit(_flip)/rev | solution.py:24
  108.9 2.8 %fusion.39 = bf16[8,512,128]{1,2,0:T(8,128)(2,1)} fusion(bf16[8,128,512]{2,1,0:T(8,128)(2,1)} %bitcast.129, bf16[8,128,512]{2,1,0:T(8,128)(2,1)S(1)} %bitcast.125, bf16[3,8,128,256]{3,2,1,0:T(8,128)(2,1)} %param.8), kind=kOutput, calls=%fused_computation.52 | convolution fusion | flops 273154048 | bytes 3670016 | tf_op jit(solution)/shard_map/bkj,bjr->bkr/dot_general | solution.py:29
  111.8 2.4 %rev.20 = bf16[1,2,4,128,512]{4,3,2,1,0:T(8,128)(2,1)} reverse(bf16[1,2,4,128,512]{4,3,2,1,0:T(8,128)(2,1)} %bitcast.126), dimensions={1} | reverse | bytes 2097152 | tf_op jit(solution)/shard_map/jit(_flip)/rev | solution.py:24
  114.1 3.2 %fusion.36 = bf16[8,512,128]{2,1,0:T(8,128)(2,1)} fusion(bf16[8,128,512]{2,1,0:T(8,128)(2,1)} %bitcast.130, bf16[8,128,512]{2,1,0:T(8,128)(2,1)S(1)} %bitcast.127, bf16[3,8,128,256]{3,2,1,0:T(8,128)(2,1)} %param.8), kind=kOutput, calls=%fused_computation.51 | convolution fusion | flops 273154048 | bytes 3670016 | tf_op jit(solution)/shard_map/bkj,bjr->bkr/dot_general | solution.py:29
  117.3 5.7 %fusion.45 = bf16[8,512,128]{2,1,0:T(8,128)(2,1)S(1)} fusion(bf16[8,1024,128]{2,1,0:T(8,128)(2,1)S(1)} %bitcast.108, bf16[8,512,128]{2,1,0:T(8,128)(2,1)} %fusion.36), kind=kOutput, calls=%fused_computation.54 | convolution fusion | flops 2152202240 | bytes 4194304 | tf_op jit(solution)/shard_map/bmk,bmr->bkr/dot_general | solution.py:66
  123.0 2.3 %convolution_convert_fusion.10 = bf16[8,512,128]{2,1,0:T(8,128)(2,1)} fusion(bf16[8,512,128]{2,1,0:T(8,128)(2,1)S(1)} %fusion.45, bf16[8,128,256]{2,1,0:T(8,128)(2,1)} %get-tuple-element.6), kind=kOutput, calls=%fused_computation.57 | convolution fusion | flops 134742016 | bytes 2359296 | tf_op jit(solution)/shard_map/bjk,bjr->bkr/dot_general | solution.py:39
  137.7 2.7 %fusion.33 = bf16[8,128,512]{1,2,0:T(8,128)(2,1)} fusion(bf16[8,128,512]{1,2,0:T(8,128)(2,1)} %bitcast.118, bf16[8,128,512]{1,2,0:T(8,128)(2,1)S(1)} %fusion.34, bf16[8,128,256]{2,1,0:T(8,128)(2,1)} %get-tuple-element.5), kind=kOutput, calls=%fused_computation.44 | convolution fusion | flops 135790592 | bytes 3407872 | tf_op jit(solution)/shard_map/bjk,bjr->bkr/dot_general | solution.py:36
  140.4 3.7 %all-to-all-start.1 = ((bf16[8,128,512]{1,2,0:T(8,128)(2,1)}), bf16[8,128,512]{1,2,0:T(8,128)(2,1)S(1)}, u32[]{:S(2)}, u32[]{:S(2)}) async-start(bf16[8,128,512]{1,2,0:T(8,128)(2,1)} %fusion.33), calls=%async_computation.1 | async-start | bytes 2097152 | tf_op jit(solution)/shard_map/all_to_all | solution.py:72
  145.2 24.0 %all-to-all-done.1 = bf16[8,128,512]{1,2,0:T(8,128)(2,1)S(1)} async-done(((bf16[8,128,512]{1,2,0:T(8,128)(2,1)}), bf16[8,128,512]{1,2,0:T(8,128)(2,1)S(1)}, u32[]{:S(2)}, u32[]{:S(2)}) %all-to-all-start.1) | async-done | bytes 1048608 | tf_op jit(solution)/shard_map/all_to_all | solution.py:72
  171.3 22.6 %collective-permute-done.3 = bf16[2,128,2048]{1,2,0:T(8,128)(2,1)S(1)} collective-permute-done((bf16[2,128,2048]{1,2,0:T(8,128)(2,1)S(1)}, bf16[2,128,2048]{1,2,0:T(8,128)(2,1)S(1)}, u32[]{:S(2)}, u32[]{:S(2)}) %collective-permute-start.3) | collective-permute-done | bytes 1048608 | tf_op jit(solution)/shard_map/ppermute | solution.py:16
  196.3 21.8 %collective-permute-done.4 = bf16[2,128,2048]{1,2,0:T(8,128)(2,1)S(1)} collective-permute-done((bf16[2,128,2048]{1,2,0:T(8,128)(2,1)S(1)}, bf16[2,128,2048]{1,2,0:T(8,128)(2,1)S(1)}, u32[]{:S(2)}, u32[]{:S(2)}) %collective-permute-start.4) | collective-permute-done | bytes 1048608 | tf_op jit(solution)/shard_map/ppermute | solution.py:16
  219.1 2.8 %collective-permute-done.5 = bf16[2,128,2048]{2,1,0:T(8,128)(2,1)} collective-permute-done((bf16[2,128,2048]{2,1,0:T(8,128)(2,1)S(1)}, bf16[2,128,2048]{2,1,0:T(8,128)(2,1)}, u32[]{:S(2)}, u32[]{:S(2)}) %collective-permute-start.5) | collective-permute-done | bytes 1048608 | tf_op jit(solution)/shard_map/ppermute | solution.py:16
  221.9 6.2 %convolution_convert_fusion = bf16[2,2048,1024]{1,2,0:T(8,128)(2,1)} fusion(bf16[2,1024,128]{2,1,0:T(8,128)(2,1)} %bitcast.113, bf16[2,128,2048]{2,1,0:T(8,128)(2,1)} %collective-permute-done.5, bf16[2,128,2048]{1,2,0:T(8,128)(2,1)S(1)} %fusion.5, bf16[2,128,256]{2,1,0:T(8,128)(2,1)S(1)} %get-tuple-element.8), kind=kOutput, calls=%fused_computation.2 | convolution fusion | flops 1213726720 | bytes 11075584 | tf_op jit(solution)/shard_map/bmk,bkr->bmr/dot_general | solution.py:76
  (39 shorter events, 25.0 us)
Async XLA Ops:
  0.0 117.3 %copy-start = (bf16[8192,128]{1,0:T(8,128)(2,1)S(1)}, bf16[8192,128]{1,0:T(8,128)(2,1)}, u32[]{:S(2)}) copy-start(bf16[8192,128]{1,0:T(8,128)(2,1)} %param.9) | copy-start | bytes 6291460
  0.0 7.9 %copy-start.7 = (bf16[3,2,128,256]{3,2,1,0:T(8,128)(2,1)S(1)}, bf16[3,2,128,256]{3,2,1,0:T(8,128)(2,1)}, u32[]{:S(2)}) copy-start(bf16[3,2,128,256]{3,2,1,0:T(8,128)(2,1)} %param.7) | copy-start | bytes 1179652
  5.0 2.8 %collective-permute-start = (bf16[2,128,2048]{2,1,0:T(8,128)(2,1)S(1)}, bf16[2,128,2048]{2,1,0:T(8,128)(2,1)S(1)}, u32[]{:S(2)}, u32[]{:S(2)}) collective-permute-start(bf16[2,128,2048]{2,1,0:T(8,128)(2,1)S(1)} %convolution_convert_fusion.7), channel_id=1, source_target_pairs={{0,4},{4,0},{8,12},{12,8},{16,20},{20,16},{24,28},{28,24},{1,5},{5... | collective-permute-start | bytes 3145736 | tf_op jit(solution)/shard_map/ppermute | solution.py:16
  8.3 26.4 %collective-permute-start.1 = (bf16[2,128,2048]{2,1,0:T(8,128)(2,1)S(1)}, bf16[2,128,2048]{2,1,0:T(8,128)(2,1)S(1)}, u32[]{:S(2)}, u32[]{:S(2)}) collective-permute-start(bf16[2,128,2048]{2,1,0:T(8,128)(2,1)S(1)} %fusion.10), channel_id=1, source_target_pairs={{0,8},{8,0},{4,12},{12,4},{16,24},{24,16},{20,28},{28,20},{1,9},{9... | collective-permute-start | bytes 3145736 | tf_op jit(solution)/shard_map/ppermute | solution.py:16
  35.2 24.7 %collective-permute-start.2 = (bf16[2,128,2048]{2,1,0:T(8,128)(2,1)S(1)}, bf16[2,128,2048]{2,1,0:T(8,128)(2,1)S(1)}, u32[]{:S(2)}, u32[]{:S(2)}) collective-permute-start(bf16[2,128,2048]{2,1,0:T(8,128)(2,1)S(1)} %fusion.11), channel_id=1, source_target_pairs={{0,16},{16,0},{4,20},{20,4},{8,24},{24,8},{12,28},{28,12},{1,17},{... | collective-permute-start | bytes 3145736 | tf_op jit(solution)/shard_map/ppermute | solution.py:16
  70.3 29.2 %all-to-all-start = ((bf16[2,128,2048]{1,0,2:T(2,128)(2,1)}), bf16[2,128,2048]{1,0,2:T(2,128)(2,1)S(1)}, u32[]{:S(2)}, u32[]{:S(2)}) async-start(bf16[2,128,2048]{1,0,2:T(2,128)(2,1)} %copy.13), calls=%async_computation | async-start | bytes 2097152 | tf_op jit(solution)/shard_map/all_to_all | solution.py:59
  101.4 2.4 %copy-start.2 = (bf16[2,128,4,512]{3,1,0,2:T(8,128)(2,1)S(1)}, bf16[2,128,4,512]{3,1,0,2:T(8,128)(2,1)}, u32[]{:S(2)}) copy-start(bf16[2,128,4,512]{3,1,0,2:T(8,128)(2,1)} %copy.14) | copy-start | bytes 3145732
  106.6 2.4 %copy-start.5 = (bf16[8,512,128]{1,2,0:T(8,128)(2,1)S(1)}, bf16[8,512,128]{1,2,0:T(8,128)(2,1)}, u32[]{:S(2)}) copy-start(bf16[8,512,128]{1,2,0:T(8,128)(2,1)} %fusion.42) | copy-start | bytes 3145732
  111.8 2.4 %copy-start.6 = (bf16[8,512,128]{1,2,0:T(8,128)(2,1)S(1)}, bf16[8,512,128]{1,2,0:T(8,128)(2,1)}, u32[]{:S(2)}) copy-start(bf16[8,512,128]{1,2,0:T(8,128)(2,1)} %fusion.39) | copy-start | bytes 3145732
  127.6 2.8 %copy-start.4 = (bf16[8,128,256]{2,1,0:T(8,128)(2,1)S(1)}, bf16[8,128,256]{2,1,0:T(8,128)(2,1)}, u32[]{:S(2)}) copy-start(bf16[8,128,256]{2,1,0:T(8,128)(2,1)} %get-tuple-element.7) | copy-start | bytes 1572868
  129.4 1.0 copy-start.1
  131.9 2.1 copy-start.3
  140.4 28.8 %all-to-all-start.1 = ((bf16[8,128,512]{1,2,0:T(8,128)(2,1)}), bf16[8,128,512]{1,2,0:T(8,128)(2,1)S(1)}, u32[]{:S(2)}, u32[]{:S(2)}) async-start(bf16[8,128,512]{1,2,0:T(8,128)(2,1)} %fusion.33), calls=%async_computation.1 | async-start | bytes 2097152 | tf_op jit(solution)/shard_map/all_to_all | solution.py:72
  169.7 24.2 %collective-permute-start.3 = (bf16[2,128,2048]{1,2,0:T(8,128)(2,1)S(1)}, bf16[2,128,2048]{1,2,0:T(8,128)(2,1)S(1)}, u32[]{:S(2)}, u32[]{:S(2)}) collective-permute-start(bf16[2,128,2048]{1,2,0:T(8,128)(2,1)S(1)} %fusion.6), channel_id=1, source_target_pairs={{0,16},{16,0},{4,20},{20,4},{8,24},{24,8},{12,28},{28,12},{1,17},{... | collective-permute-start | bytes 3145736 | tf_op jit(solution)/shard_map/ppermute | solution.py:16
  194.7 23.4 %collective-permute-start.4 = (bf16[2,128,2048]{1,2,0:T(8,128)(2,1)S(1)}, bf16[2,128,2048]{1,2,0:T(8,128)(2,1)S(1)}, u32[]{:S(2)}, u32[]{:S(2)}) collective-permute-start(bf16[2,128,2048]{1,2,0:T(8,128)(2,1)S(1)} %fusion.7), channel_id=1, source_target_pairs={{0,8},{8,0},{4,12},{12,4},{16,24},{24,16},{20,28},{28,20},{1,9},{9... | collective-permute-start | bytes 3145736 | tf_op jit(solution)/shard_map/ppermute | solution.py:16
  219.0 2.9 %collective-permute-start.5 = (bf16[2,128,2048]{2,1,0:T(8,128)(2,1)S(1)}, bf16[2,128,2048]{2,1,0:T(8,128)(2,1)}, u32[]{:S(2)}, u32[]{:S(2)}) collective-permute-start(bf16[2,128,2048]{2,1,0:T(8,128)(2,1)S(1)} %fusion.8), channel_id=1, source_target_pairs={{0,4},{4,0},{8,12},{12,8},{16,20},{20,16},{24,28},{28,24},{1,5},{5... | collective-permute-start | bytes 3145736 | tf_op jit(solution)/shard_map/ppermute | solution.py:16
where the time goes:
time: 229 us; the launch traced here: 228 us
  waiting for transfers between devices  142 us (62%)
  matrix products  40.4 us (18%)
  local copies, waits for them, and re-layouts  28.8 us (13%)
  starting transfers between devices  17.1 us (7%)
    ppermute x6, waiting for transfers between devices, swapped(): return lax.ppermute(block, axis, route)  95.8 us
    all_to_all x1, waiting for transfers between devices, body(): lax.all_to_all(gradient, 'row', split_axis=0, concat_axis=2, tiled=True)  24 us
    all_to_all x1, waiting for transfers between devices, body(): lax.all_to_all(coeffs, 'row', split_axis=2, concat_axis=0, tiled=True)  21.8 us
    dot_general x6, matrix products, forward_mix(): jnp.einsum('bkj,bjr->bkr', weights, stacked, preferred_element_type=jnp.f...  10.6 us
    rev x5, local copies, waits for them, and re-layouts, partner_of(): return jnp.flip(shaped, 1).reshape(coeffs.shape)  10.3 us
    convert_element_type x1, local copies, waits for them, and re-layouts, forward_mix(): jnp.einsum('bkj,bjr->bkr', weights, stacked, preferred_element_type=jnp.f...  9.46 us
    ppermute x6, starting transfers between devices, swapped(): return lax.ppermute(block, axis, route)  8.57 us
    dot_general x5, matrix products, backward_terms(): jnp.einsum('bjk,bjr->bkr', weights[:, :, :rank_size], gradient, preferred...  7.42 us
  transfers between devices with their start and end apart: 8, of which 8 were waited for; matrix products, arithmetic and copies ran while one was open for 2% of the time, Pallas kernels for 0%

commit v1 on v0

--- a/solution.py
+++ b/solution.py
@@ -56,7 +56,10 @@
     for level_bit in range(col_bits):
         partner = swapped(coeffs, "col", level_bit)
         coeffs = forward_mix(mix_in[level_bit], coeffs, partner)
-    coeffs = lax.all_to_all(coeffs, "row", split_axis=2, concat_axis=0, tiled=True)
+    peers = lax.axis_size("row")
+    parts = jnp.stack(jnp.split(coeffs, peers, axis=2), axis=0)
+    parts = lax.all_to_all(parts, "row", split_axis=0, concat_axis=0)
+    coeffs = jnp.concatenate(parts, axis=0)
     for level_bit in range(row_bits + 1):
         coeffs = forward_mix(mix_out[level_bit], coeffs, partner_of(coeffs, level_bit))
     out_rows = leaf_out.reshape(-1, LEAF_SIZE, rank_size)

time: 229 us -> 221 us (0.965)
  local copies, waits for them, and re-layouts: 28.8 us -> 19.8 us
    convert_element_type x1 -> x0, local copies, waits for them, and re-layouts: 9.46 us -> none  [forward_mix(): jnp.einsum('bkj,bjr->bkr', weights, stacked, preferred_element_type=jnp.f...]
    reshape x0 -> x2, local copies, waits for them, and re-layouts: none -> 3.69 us  [the longest x1 2.35 us: partner_of(): return jnp.flip(shaped, 1).reshape(coeffs.shape)]
where the time goes in v1:
time: 221 us; the launch traced here: 220 us
  waiting for transfers between devices  142 us (64%)
  matrix products  40.4 us (18%)
  local copies, waits for them, and re-layouts  19.8 us (9%)
  starting transfers between devices  17.1 us (8%)
    ppermute x6, waiting for transfers between devices, swapped(): return lax.ppermute(block, axis, route)  95.8 us
    all_to_all x1, waiting for transfers between devices, body(): lax.all_to_all(gradient, 'row', split_axis=0, concat_axis=2, tiled=True)  24 us
    all_to_all x1, waiting for transfers between devices, body(): parts = lax.all_to_all(parts, 'row', split_axis=0, concat_axis=0)  21.8 us
    dot_general x6, matrix products, forward_mix(): jnp.einsum('bkj,bjr->bkr', weights, stacked, preferred_element_type=jnp.f...  10.6 us
    rev x5, local copies, waits for them, and re-layouts, partner_of(): return jnp.flip(shaped, 1).reshape(coeffs.shape)  10.4 us
    ppermute x6, starting transfers between devices, swapped(): return lax.ppermute(block, axis, route)  8.54 us
    dot_general x5, matrix products, backward_terms(): jnp.einsum('bjk,bjr->bkr', weights[:, :, :rank_size], gradient, preferred...  7.42 us
    dot_general x1, matrix products, body(): jnp.einsum('bmk,bkr->bmr', leaf_rows, gradient, preferred_element_type=jn...  6.18 us
  transfers between devices with their start and end apart: 8, of which 8 were waited for; matrix products, arithmetic and copies ran while one was open for 2% of the time, Pallas kernels for 0%

profile of v1, /device:TPU:0, one launch (start us, length us, event | category | flops | bytes accessed | tf_op | source)
XLA Modules:
  0.0 220.2 jit_solution(18189421913028967174)
XLA Ops:
  0.0 5.0 %convolution_convert_fusion.7 = bf16[2,128,2048]{2,1,0:T(8,128)(2,1)S(1)} fusion(bf16[2,1024,128]{2,1,0:T(8,128)(2,1)} %bitcast.118, bf16[2,1024,2048]{2,1,0:T(8,128)(2,1)} %bitcast.114), kind=kOutput, calls=%fused_computation.15 | convolution fusion | flops 1074266112 | bytes 9961472 | tf_op jit(solution)/shard_map/bmk,bmr->bkr/dot_general | solution.py:53
  8.3 2.9 %collective-permute-start.1 = (bf16[2,128,2048]{2,1,0:T(8,128)(2,1)S(1)}, bf16[2,128,2048]{2,1,0:T(8,128)(2,1)S(1)}, u32[]{:S(2)}, u32[]{:S(2)}) collective-permute-start(bf16[2,128,2048]{2,1,0:T(8,128)(2,1)S(1)} %fusion.10), channel_id=1, source_target_pairs={{0,8},{8,0},{4,12},{12,4},{16,24},{24,16},{20,28},{28,20},{1,9},{9... | collective-permute-start | bytes 3145736 | tf_op jit(solution)/shard_map/ppermute | solution.py:16
  11.2 23.5 %collective-permute-done.1 = bf16[2,128,2048]{2,1,0:T(8,128)(2,1)S(1)} collective-permute-done((bf16[2,128,2048]{2,1,0:T(8,128)(2,1)S(1)}, bf16[2,128,2048]{2,1,0:T(8,128)(2,1)S(1)}, u32[]{:S(2)}, u32[]{:S(2)}) %collective-permute-start.1) | collective-permute-done | bytes 1048608 | tf_op jit(solution)/shard_map/ppermute | solution.py:16
  37.0 22.9 %collective-permute-done.2 = bf16[2,128,2048]{2,1,0:T(8,128)(2,1)S(1)} collective-permute-done((bf16[2,128,2048]{2,1,0:T(8,128)(2,1)S(1)}, bf16[2,128,2048]{2,1,0:T(8,128)(2,1)S(1)}, u32[]{:S(2)}, u32[]{:S(2)}) %collective-permute-start.2) | collective-permute-done | bytes 1048608 | tf_op jit(solution)/shard_map/ppermute | solution.py:16
  62.0 4.8 %all-to-all-start = ((bf16[4,2,128,512]{2,3,1,0:T(8,128)(2,1)}), bf16[4,2,128,512]{2,3,1,0:T(8,128)(2,1)S(1)}, u32[]{:S(2)}, u32[]{:S(2)}) async-start(bf16[4,2,128,512]{2,3,1,0:T(8,128)(2,1)} %pad_maximum_fusion), calls=%async_computation | async-start | bytes 2097152 | tf_op jit(solution)/shard_map/all_to_all | solution.py:61
  66.8 2.5 %slice_bitcast_fusion.2 = (bf16[8,128,256]{2,1,0:T(8,128)(2,1)}, bf16[8,128,256]{2,1,0:T(8,128)(2,1)}, bf16[8,128,256]{2,1,0:T(8,128)(2,1)}) fusion(bf16[3,8,128,256]{3,2,1,0:T(8,128)(2,1)} %param.8), kind=kLoop, calls=%fused_computation.61 | loop fusion | bytes 3145728 | tf_op jit(solution)/shard_map/squeeze | solution.py:73
  69.4 21.8 %all-to-all-done = bf16[4,2,128,512]{2,3,1,0:T(8,128)(2,1)S(1)} async-done(((bf16[4,2,128,512]{2,3,1,0:T(8,128)(2,1)}), bf16[4,2,128,512]{2,3,1,0:T(8,128)(2,1)S(1)}, u32[]{:S(2)}, u32[]{:S(2)}) %all-to-all-start) | async-done | bytes 1048608 | tf_op jit(solution)/shard_map/all_to_all | solution.py:61
  93.5 2.4 %copy.9 = bf16[8,128,512]{2,1,0:T(8,128)(2,1)} copy(bf16[8,128,512]{1,2,0:T(8,128)(2,1)} %bitcast.124) | data formatting | bytes 2097152 | tf_op jit(solution)/shard_map/reshape | solution.py:24
  95.9 2.8 %fusion.42 = bf16[8,512,128]{1,2,0:T(8,128)(2,1)} fusion(bf16[8,128,512]{2,1,0:T(8,128)(2,1)} %copy.9, bf16[8,128,512]{2,1,0:T(8,128)(2,1)S(1)} %copy-done.4, bf16[3,8,128,256]{3,2,1,0:T(8,128)(2,1)} %param.8), kind=kOutput, calls=%fused_computation.53 | convolution fusion | flops 273154048 | bytes 3670016 | tf_op jit(solution)/shard_map/bkj,bjr->bkr/dot_general | solution.py:29
  98.7 2.4 %rev.19 = bf16[2,2,2,128,512]{4,3,2,1,0:T(8,128)(2,1)} reverse(bf16[2,2,2,128,512]{4,3,2,1,0:T(8,128)(2,1)} %bitcast.128), dimensions={1} | reverse | bytes 2097152 | tf_op jit(solution)/shard_map/jit(_flip)/rev | solution.py:24
  101.1 2.8 %fusion.39 = bf16[8,512,128]{1,2,0:T(8,128)(2,1)} fusion(bf16[8,128,512]{2,1,0:T(8,128)(2,1)} %bitcast.132, bf16[8,128,512]{2,1,0:T(8,128)(2,1)S(1)} %bitcast.129, bf16[3,8,128,256]{3,2,1,0:T(8,128)(2,1)} %param.8), kind=kOutput, calls=%fused_computation.52 | convolution fusion | flops 273154048 | bytes 3670016 | tf_op jit(solution)/shard_map/bkj,bjr->bkr/dot_general | solution.py:29
  103.9 2.4 %rev.20 = bf16[1,2,4,128,512]{4,3,2,1,0:T(8,128)(2,1)} reverse(bf16[1,2,4,128,512]{4,3,2,1,0:T(8,128)(2,1)} %bitcast.130), dimensions={1} | reverse | bytes 2097152 | tf_op jit(solution)/shard_map/jit(_flip)/rev | solution.py:24
  106.3 3.2 %fusion.36 = bf16[8,512,128]{2,1,0:T(8,128)(2,1)} fusion(bf16[8,128,512]{2,1,0:T(8,128)(2,1)} %bitcast.133, bf16[8,128,512]{2,1,0:T(8,128)(2,1)S(1)} %bitcast.131, bf16[3,8,128,256]{3,2,1,0:T(8,128)(2,1)} %param.8), kind=kOutput, calls=%fused_computation.51 | convolution fusion | flops 273154048 | bytes 3670016 | tf_op jit(solution)/shard_map/bkj,bjr->bkr/dot_general | solution.py:29
  109.4 5.7 %fusion.45 = bf16[8,512,128]{2,1,0:T(8,128)(2,1)S(1)} fusion(bf16[8,1024,128]{2,1,0:T(8,128)(2,1)S(1)} %bitcast.113, bf16[8,512,128]{2,1,0:T(8,128)(2,1)} %fusion.36), kind=kOutput, calls=%fused_computation.54 | convolution fusion | flops 2152202240 | bytes 4194304 | tf_op jit(solution)/shard_map/bmk,bmr->bkr/dot_general | solution.py:69
  115.2 2.3 %convolution_convert_fusion.10 = bf16[8,512,128]{2,1,0:T(8,128)(2,1)} fusion(bf16[8,512,128]{2,1,0:T(8,128)(2,1)S(1)} %fusion.45, bf16[8,128,256]{2,1,0:T(8,128)(2,1)} %get-tuple-element.6), kind=kOutput, calls=%fused_computation.57 | convolution fusion | flops 134742016 | bytes 2359296 | tf_op jit(solution)/shard_map/bjk,bjr->bkr/dot_general | solution.py:39
  117.5 2.3 %rev.21 = bf16[1,2,4,128,512]{3,4,2,1,0:T(8,128)(2,1)} reverse(bf16[1,2,4,128,512]{3,4,2,1,0:T(8,128)(2,1)} %bitcast.125), dimensions={1} | reverse | bytes 2097152 | tf_op jit(solution)/shard_map/jit(_flip)/rev | solution.py:24
  127.6 2.3 %rev.23 = bf16[4,2,1,128,512]{3,4,1,0,2:T(8,128)(2,1)} reverse(bf16[4,2,1,128,512]{3,4,1,0,2:T(8,128)(2,1)} %bitcast.127), dimensions={1} | reverse | bytes 2097152 | tf_op jit(solution)/shard_map/jit(_flip)/rev | solution.py:24
  129.9 2.7 %fusion.33 = bf16[8,128,512]{1,2,0:T(8,128)(2,1)} fusion(bf16[8,128,512]{1,2,0:T(8,128)(2,1)} %bitcast.123, bf16[8,128,512]{1,2,0:T(8,128)(2,1)S(1)} %fusion.34, bf16[8,128,256]{2,1,0:T(8,128)(2,1)} %get-tuple-element.5), kind=kOutput, calls=%fused_computation.44 | convolution fusion | flops 135790592 | bytes 3407872 | tf_op jit(solution)/shard_map/bjk,bjr->bkr/dot_general | solution.py:36
  132.6 3.7 %all-to-all-start.1 = ((bf16[8,128,512]{1,2,0:T(8,128)(2,1)}), bf16[8,128,512]{1,2,0:T(8,128)(2,1)S(1)}, u32[]{:S(2)}, u32[]{:S(2)}) async-start(bf16[8,128,512]{1,2,0:T(8,128)(2,1)} %fusion.33), calls=%async_computation.1 | async-start | bytes 2097152 | tf_op jit(solution)/shard_map/all_to_all | solution.py:75
  137.4 24.0 %all-to-all-done.1 = bf16[8,128,512]{1,2,0:T(8,128)(2,1)S(1)} async-done(((bf16[8,128,512]{1,2,0:T(8,128)(2,1)}), bf16[8,128,512]{1,2,0:T(8,128)(2,1)S(1)}, u32[]{:S(2)}, u32[]{:S(2)}) %all-to-all-start.1) | async-done | bytes 1048608 | tf_op jit(solution)/shard_map/all_to_all | solution.py:75
  163.4 22.7 %collective-permute-done.3 = bf16[2,128,2048]{1,2,0:T(8,128)(2,1)S(1)} collective-permute-done((bf16[2,128,2048]{1,2,0:T(8,128)(2,1)S(1)}, bf16[2,128,2048]{1,2,0:T(8,128)(2,1)S(1)}, u32[]{:S(2)}, u32[]{:S(2)}) %collective-permute-start.3) | collective-permute-done | bytes 1048608 | tf_op jit(solution)/shard_map/ppermute | solution.py:16
  188.5 21.8 %collective-permute-done.4 = bf16[2,128,2048]{1,2,0:T(8,128)(2,1)S(1)} collective-permute-done((bf16[2,128,2048]{1,2,0:T(8,128)(2,1)S(1)}, bf16[2,128,2048]{1,2,0:T(8,128)(2,1)S(1)}, u32[]{:S(2)}, u32[]{:S(2)}) %collective-permute-start.4) | collective-permute-done | bytes 1048608 | tf_op jit(solution)/shard_map/ppermute | solution.py:16
  211.3 2.8 %collective-permute-done.5 = bf16[2,128,2048]{2,1,0:T(8,128)(2,1)} collective-permute-done((bf16[2,128,2048]{2,1,0:T(8,128)(2,1)S(1)}, bf16[2,128,2048]{2,1,0:T(8,128)(2,1)}, u32[]{:S(2)}, u32[]{:S(2)}) %collective-permute-start.5) | collective-permute-done | bytes 1048608 | tf_op jit(solution)/shard_map/ppermute | solution.py:16
  214.1 6.2 %convolution_convert_fusion = bf16[2,2048,1024]{1,2,0:T(8,128)(2,1)} fusion(bf16[2,1024,128]{2,1,0:T(8,128)(2,1)} %bitcast.119, bf16[2,128,2048]{2,1,0:T(8,128)(2,1)} %collective-permute-done.5, bf16[2,128,2048]{1,2,0:T(8,128)(2,1)S(1)} %fusion.5, bf16[2,128,256]{2,1,0:T(8,128)(2,1)S(1)} %get-tuple-element.12), kind=kOutput, calls=%fused_computation.2 | convolution fusion | flops 1213726720 | bytes 11075584 | tf_op jit(solution)/shard_map/bmk,bkr->bmr/dot_general | solution.py:79
  (41 shorter events, 24.3 us)
Async XLA Ops:
  0.0 109.4 %copy-start = (bf16[8192,128]{1,0:T(8,128)(2,1)S(1)}, bf16[8192,128]{1,0:T(8,128)(2,1)}, u32[]{:S(2)}) copy-start(bf16[8192,128]{1,0:T(8,128)(2,1)} %param.9) | copy-start | bytes 6291460
  0.0 7.9 %copy-start.7 = (bf16[3,2,128,256]{3,2,1,0:T(8,128)(2,1)S(1)}, bf16[3,2,128,256]{3,2,1,0:T(8,128)(2,1)}, u32[]{:S(2)}) copy-start(bf16[3,2,128,256]{3,2,1,0:T(8,128)(2,1)} %param.7) | copy-start | bytes 1179652
  5.0 2.8 %collective-permute-start = (bf16[2,128,2048]{2,1,0:T(8,128)(2,1)S(1)}, bf16[2,128,2048]{2,1,0:T(8,128)(2,1)S(1)}, u32[]{:S(2)}, u32[]{:S(2)}) collective-permute-start(bf16[2,128,2048]{2,1,0:T(8,128)(2,1)S(1)} %convolution_convert_fusion.7), channel_id=1, source_target_pairs={{0,4},{4,0},{8,12},{12,8},{16,20},{20,16},{24,28},{28,24},{1,5},{5... | collective-permute-start | bytes 3145736 | tf_op jit(solution)/shard_map/ppermute | solution.py:16
  8.3 26.4 %collective-permute-start.1 = (bf16[2,128,2048]{2,1,0:T(8,128)(2,1)S(1)}, bf16[2,128,2048]{2,1,0:T(8,128)(2,1)S(1)}, u32[]{:S(2)}, u32[]{:S(2)}) collective-permute-start(bf16[2,128,2048]{2,1,0:T(8,128)(2,1)S(1)} %fusion.10), channel_id=1, source_target_pairs={{0,8},{8,0},{4,12},{12,4},{16,24},{24,16},{20,28},{28,20},{1,9},{9... | collective-permute-start | bytes 3145736 | tf_op jit(solution)/shard_map/ppermute | solution.py:16
  35.2 24.7 %collective-permute-start.2 = (bf16[2,128,2048]{2,1,0:T(8,128)(2,1)S(1)}, bf16[2,128,2048]{2,1,0:T(8,128)(2,1)S(1)}, u32[]{:S(2)}, u32[]{:S(2)}) collective-permute-start(bf16[2,128,2048]{2,1,0:T(8,128)(2,1)S(1)} %fusion.11), channel_id=1, source_target_pairs={{0,16},{16,0},{4,20},{20,4},{8,24},{24,8},{12,28},{28,12},{1,17},{... | collective-permute-start | bytes 3145736 | tf_op jit(solution)/shard_map/ppermute | solution.py:16
  62.0 29.2 %all-to-all-start = ((bf16[4,2,128,512]{2,3,1,0:T(8,128)(2,1)}), bf16[4,2,128,512]{2,3,1,0:T(8,128)(2,1)S(1)}, u32[]{:S(2)}, u32[]{:S(2)}) async-start(bf16[4,2,128,512]{2,3,1,0:T(8,128)(2,1)} %pad_maximum_fusion), calls=%async_computation | async-start | bytes 2097152 | tf_op jit(solution)/shard_map/all_to_all | solution.py:61
  93.5 2.4 %copy-start.4 = (bf16[8,128,512]{2,1,0:T(8,128)(2,1)S(1)}, bf16[8,128,512]{2,1,0:T(8,128)(2,1)}, u32[]{:S(2)}) copy-start(bf16[8,128,512]{2,1,0:T(8,128)(2,1)} %copy.8) | copy-start | bytes 3145732
  98.7 2.4 %copy-start.5 = (bf16[8,512,128]{1,2,0:T(8,128)(2,1)S(1)}, bf16[8,512,128]{1,2,0:T(8,128)(2,1)}, u32[]{:S(2)}) copy-start(bf16[8,512,128]{1,2,0:T(8,128)(2,1)} %fusion.42) | copy-start | bytes 3145732
  103.9 2.4 %copy-start.6 = (bf16[8,512,128]{1,2,0:T(8,128)(2,1)S(1)}, bf16[8,512,128]{1,2,0:T(8,128)(2,1)}, u32[]{:S(2)}) copy-start(bf16[8,512,128]{1,2,0:T(8,128)(2,1)} %fusion.39) | copy-start | bytes 3145732
  119.8 2.8 %copy-start.3 = (bf16[8,128,256]{2,1,0:T(8,128)(2,1)S(1)}, bf16[8,128,256]{2,1,0:T(8,128)(2,1)}, u32[]{:S(2)}) copy-start(bf16[8,128,256]{2,1,0:T(8,128)(2,1)} %get-tuple-element.7) | copy-start | bytes 1572868
  121.6 1.0 copy-start.1
  124.0 2.1 copy-start.2
  132.6 28.8 %all-to-all-start.1 = ((bf16[8,128,512]{1,2,0:T(8,128)(2,1)}), bf16[8,128,512]{1,2,0:T(8,128)(2,1)S(1)}, u32[]{:S(2)}, u32[]{:S(2)}) async-start(bf16[8,128,512]{1,2,0:T(8,128)(2,1)} %fusion.33), calls=%async_computation.1 | async-start | bytes 2097152 | tf_op jit(solution)/shard_map/all_to_all | solution.py:75
  161.8 24.2 %collective-permute-start.3 = (bf16[2,128,2048]{1,2,0:T(8,128)(2,1)S(1)}, bf16[2,128,2048]{1,2,0:T(8,128)(2,1)S(1)}, u32[]{:S(2)}, u32[]{:S(2)}) collective-permute-start(bf16[2,128,2048]{1,2,0:T(8,128)(2,1)S(1)} %fusion.6), channel_id=1, source_target_pairs={{0,16},{16,0},{4,20},{20,4},{8,24},{24,8},{12,28},{28,12},{1,17},{... | collective-permute-start | bytes 3145736 | tf_op jit(solution)/shard_map/ppermute | solution.py:16
  186.9 23.4 %collective-permute-start.4 = (bf16[2,128,2048]{1,2,0:T(8,128)(2,1)S(1)}, bf16[2,128,2048]{1,2,0:T(8,128)(2,1)S(1)}, u32[]{:S(2)}, u32[]{:S(2)}) collective-permute-start(bf16[2,128,2048]{1,2,0:T(8,128)(2,1)S(1)} %fusion.7), channel_id=1, source_target_pairs={{0,8},{8,0},{4,12},{12,4},{16,24},{24,16},{20,28},{28,20},{1,9},{9... | collective-permute-start | bytes 3145736 | tf_op jit(solution)/shard_map/ppermute | solution.py:16
  211.2 2.9 %collective-permute-start.5 = (bf16[2,128,2048]{2,1,0:T(8,128)(2,1)S(1)}, bf16[2,128,2048]{2,1,0:T(8,128)(2,1)}, u32[]{:S(2)}, u32[]{:S(2)}) collective-permute-start(bf16[2,128,2048]{2,1,0:T(8,128)(2,1)S(1)} %fusion.8), channel_id=1, source_target_pairs={{0,4},{4,0},{8,12},{12,8},{16,20},{20,16},{24,28},{28,24},{1,5},{5... | collective-permute-start | bytes 3145736 | tf_op jit(solution)/shard_map/ppermute | solution.py:16
